TPU v7x, 32 devices: a whole 2x2x4 slice. The times are simulated.
32 devices in a mesh: rep: 2 (over y), gx: 4 (over x, core), gy: 4 (over z).
Axes of the slice: x: 2, y: 2, z: 4, core: 2. Of those that a mesh axis runs over, the one named last changes fastest.
Arguments:
- deltas: bfloat16 [2, 2, 3584, 14336], P('rep', None, 'gx', 'gy'), may hold values from -32 to 32
- params: float32 [2, 4, 4, 2, 4, 4, 112, 896], P(None, None, 'gx', 'rep', None, 'gy'), may hold values from -0.75 to 0.75
- momentum: float32 [2, 4, 4, 2, 4, 4, 112, 896], P(None, None, 'gx', 'rep', None, 'gy'), may hold values from -1.5 to 1.5
Outputs:
- new_params: float32 [2, 4, 4, 2, 4, 4, 112, 896], P(None, None, 'gx', 'rep', None, 'gy')
- new_momentum: float32 [2, 4, 4, 2, 4, 4, 112, 896], P(None, None, 'gx', 'rep', None, 'gy')
All inputs are finite; a program needn't handle non-finite values.
Results may differ from a plain program's by a relative error of at most 0.0003.
Values may be sent and summed in bfloat16 or wider, within the bound.
A program may use at most 128 MiB of HBM per device.

v0:
```python
import jax
import jax.numpy as jnp
from jax import lax
from jax.sharding import PartitionSpec as P

clip_level = 0.25
moment_decay = 0.9
outer_rate = 0.7
epsilon = 1e-06


def per_device(deltas, params, momentum):
    rows_split = lax.axis_size("gx")
    cols_split = lax.axis_size("gy")
    replicas = lax.axis_size("rep")
    matrices = deltas.shape[1]
    local_rows = deltas.shape[2]
    local_cols = deltas.shape[3]
    row_tile = local_rows // (rows_split * replicas)
    col_tile = local_cols // cols_split
    entries = matrices * local_rows * local_cols * rows_split * cols_split
    blocks = deltas.reshape(matrices, rows_split, replicas, row_tile, cols_split, col_tile)
    received = lax.all_to_all(blocks[None], "rep", split_axis=3, concat_axis=0, tiled=True)
    summed = jnp.sum(received, axis=0, dtype=jnp.float32)
    partial_value = summed / replicas
    squares = lax.psum(jnp.sum(partial_value * partial_value), ("rep", "gx", "gy"))
    mean_delta = lax.all_to_all(
        lax.all_to_all(partial_value, "gx", split_axis=1, concat_axis=1, tiled=True),
        "gy",
        split_axis=4,
        concat_axis=4,
        tiled=True,
    )
    root_mean = jnp.sqrt(squares / entries + epsilon)
    clip_scale = jnp.minimum(1.0, clip_level / root_mean)
    arranged = jnp.transpose(mean_delta, (0, 1, 2, 4, 3, 5)).reshape(params.shape)
    gradient = clip_scale * arranged
    new_momentum = moment_decay * momentum + gradient
    new_params = params - outer_rate * (gradient + moment_decay * new_momentum)
    return (new_params, new_momentum)


def solution(mesh):
    return jax.shard_map(
        per_device,
        mesh=mesh,
        in_specs=(
            P("rep", None, "gx", "gy"),
            P(None, None, "gx", "rep", None, "gy", None, None),
            P(None, None, "gx", "rep", None, "gy", None, None),
        ),
        out_specs=(
            P(None, None, "gx", "rep", None, "gy", None, None),
            P(None, None, "gx", "rep", None, "gy", None, None),
        ),
        check_vma=False,
    )
```

profile of v0, /device:TPU:0, one launch (start us, length us, event | category | flops | bytes accessed | tf_op | source)
XLA Modules:
  0.0 728.3 jit_solution(14214572394206877874)
XLA Ops:
  0.6 21.9 %broadcast_in_dim_reshape.3 = bf16[1,2,4,2,112,4,896]{6,5,4,3,2,1,0:T(4,128)(2,1)} reshape(bf16[1,2,896,3584]{3,2,1,0:T(8,128)(2,1)} %param.3) | data formatting | bytes 25690112 | tf_op jit(solution)/shard_map/broadcast_in_dim;reshape | solution.py:23
  22.6 7.8 %copy.20 = bf16[1,2,4,2,112,4,896]{6,5,4,2,1,0,3:T(4,128)(2,1)S(1)} copy(bf16[1,2,4,2,112,4,896]{6,5,4,3,2,1,0:T(4,128)(2,1)} %broadcast_in_dim_reshape.3) | data formatting | bytes 25690112 | tf_op jit(solution)/shard_map/broadcast_in_dim;reshape | solution.py:23
  30.4 146.6 %all_to_all.19 = bf16[1,2,4,2,112,4,896]{6,5,4,2,1,0,3:T(4,128)(2,1)} all-to-all(bf16[1,2,4,2,112,4,896]{6,5,4,2,1,0,3:T(4,128)(2,1)S(1)} %copy.20), channel_id=1, replica_groups=mesh['rep'=2,'gx'=4,'gy'=4] {'rep'}, dimensions={3} | all-to-all | bytes 25690112 | tf_op jit(solution)/shard_map/all_to_all | solution.py:23
  177.0 15.0 %convert_reduce_fusion = f32[2,4,112,4,896]{4,2,3,1,0:T(8,128)} fusion(bf16[1,2,4,2,112,4,896]{6,5,4,2,1,0,3:T(4,128)(2,1)} %all_to_all.19), kind=kLoop, calls=%fused_computation | loop fusion | flops 9633792 | bytes 25690112 | tf_op jit(solution)/shard_map/reduce_sum | solution.py:24
  192.1 15.7 %multiply_reduce_fusion = (f32[]{:T(128)}, f32[2,4,1,112,4,896]{5,4,3,1,0,2:T(4,128)}) fusion(f32[2,4,112,4,896]{4,2,3,1,0:T(8,128)} %convert_reduce_fusion), kind=kLoop, calls=%fused_computation.7 | loop fusion | flops 9633791 | bytes 25690116 | tf_op jit(solution)/shard_map/reduce_sum | solution.py:26
  207.8 10.6 %copy.23 = f32[2,4,1,112,4,896]{5,3,4,0,2,1:T(8,128)} copy(f32[2,4,1,112,4,896]{5,4,3,1,0,2:T(4,128)} %get-tuple-element.11) | data formatting | bytes 25690112 | tf_op jit(solution)/shard_map/div | solution.py:25
  218.5 150.4 %all_to_all.20 = f32[2,4,1,112,4,896]{5,3,4,0,2,1:T(8,128)} all-to-all(f32[2,4,1,112,4,896]{5,3,4,0,2,1:T(8,128)} %copy.23), channel_id=1, replica_groups=mesh['rep'=2,'gx'=4,'gy'=4] {'gx'}, dimensions={1} | all-to-all | bytes 25690112 | tf_op jit(solution)/shard_map/all_to_all | solution.py:28
  368.9 10.6 %copy.24 = f32[2,4,1,112,4,896]{5,3,1,0,2,4:T(8,128)} copy(f32[2,4,1,112,4,896]{5,3,4,0,2,1:T(8,128)} %all_to_all.20) | data formatting | bytes 25690112 | tf_op jit(solution)/shard_map/all_to_all | solution.py:28
  379.5 6.4 all-to-all-start.2
  385.9 298.0 %psum.7 = f32[]{:T(128)} all-reduce(f32[]{:T(128)} %get-tuple-element.10), channel_id=1, replica_groups=mesh['rep'=2,'gx'=4,'gy'=4] {'rep','gx','gy'}, use_global_device_ids=true, to_apply=%region_2.0 | all-reduce | flops 1 | bytes 8 | tf_op jit(solution)/shard_map/psum | solution.py:26
  684.6 0.0 all-to-all-done.2
  684.6 22.3 %bitcast_add_fusion.1 = (f32[2,4,1,1,4,1,112,896]{7,6,1,0,4,5,3,2:T(8,128)}, f32[2,4,1,1,4,1,112,896]{7,6,1,0,4,5,3,2:T(8,128)}) fusion(f32[2,4,1,1,4,1,112,896]{7,6,5,4,3,2,1,0:T(8,128)} %param.5, f32[2,4,1,112,4,896]{5,3,1,0,2,4:T(8,128)} %all-to-all-done.2, f32[]{:T(128)S(6)} %min_shard_map.3, f32[2,4,1,1,4,1,112,896]{7,6,5,4,3,2,1,0:T(8,128)} %param.4), kind=kLoop, calls=%fused_computation.3 | loop fusion | flops 22478848 | bytes 64225284 | tf_op jit(solution)/shard_map/add | solution.py:38
  706.9 10.7 %copy.28 = f32[2,4,1,1,4,1,112,896]{7,6,5,4,3,2,1,0:T(8,128)} copy(f32[2,4,1,1,4,1,112,896]{7,6,1,0,4,5,3,2:T(8,128)} %get-tuple-element.8) | data formatting | bytes 25690112
  717.6 10.7 %copy.27 = f32[2,4,1,1,4,1,112,896]{7,6,5,4,3,2,1,0:T(8,128)} copy(f32[2,4,1,1,4,1,112,896]{7,6,1,0,4,5,3,2:T(8,128)} %get-tuple-element.9) | data formatting | bytes 25690112
Async XLA Ops:
  379.5 305.1 %all-to-all-start.2 = ((f32[2,4,1,112,4,896]{5,3,1,0,2,4:T(8,128)}), f32[2,4,1,112,4,896]{5,3,1,0,2,4:T(8,128)}, u32[]{:S(2)}, u32[]{:S(2)}) async-start(f32[2,4,1,112,4,896]{5,3,1,0,2,4:T(8,128)} %copy.24), calls=%async_computation.2 | async-start | bytes 25690112 | tf_op jit(solution)/shard_map/all_to_all | solution.py:27
where the time goes:
time: 730 us; the launch traced here: 728 us
  blocking collectives  595 us (82%)
  local copies, waits for them, and re-layouts  72.4 us (10%)
  other arithmetic  53.1 us (7%)
    psum x1, blocking collectives, per_device(): lax.psum(jnp.sum(partial_value * partial_value), ('rep', 'gx', 'gy'))  298 us
    all_to_all x1, blocking collectives, per_device(): lax.all_to_all(partial_value, 'gx', split_axis=1, concat_axis=1, tiled=True)  150 us
    all_to_all x1, blocking collectives, per_device(): lax.all_to_all(blocks[None], 'rep', split_axis=3, concat_axis=0, tiled=True)  147 us
    another operation x2, local copies, waits for them, and re-layouts, per_device(): blocks[None]  29.8 us
    add x1, other arithmetic, per_device(): new_momentum = moment_decay * momentum + gradient  22.3 us
    unnamed x2, local copies, waits for them, and re-layouts  21.4 us
    reduce_sum x1, other arithmetic, per_device(): jnp.sum(partial_value * partial_value)  15.7 us
    reduce_sum x1, other arithmetic, per_device(): summed = jnp.sum(received, axis=0, dtype=jnp.float32)  15 us
  transfers between devices with their start and end apart: 1, of which 0 were waited for; matrix products, arithmetic and copies ran while one was open for 0% of the time, Pallas kernels for 0%

commit v1 on v0

v1 whole, which is shorter than its diff:
```python
import functools

import jax
import jax.numpy as jnp
from jax import lax
from jax.experimental import pallas as pl
from jax.experimental.pallas import tpu as pltpu
from jax.sharding import PartitionSpec as P

clip_level = 0.25
moment_decay = 0.9
outer_rate = 0.7
epsilon = 1e-06

MESH = pl.DeviceIdType.MESH
LANES = 128
TOP = 240.0
SMALLEST = 1e-30
AHEAD = 6


def encode(value):
    power = value * value
    for _ in range(3):
        power = power * power
    return jnp.where(value < 0.0, -power, power).astype(jnp.bfloat16)


def decode(code):
    wide = code.astype(jnp.float32)
    root = jnp.abs(wide)
    for _ in range(4):
        root = lax.rsqrt(root)
    root = jnp.where(wide == 0.0, 0.0, root)
    return jnp.where(wide < 0.0, -root, root)


def fold_lanes(tile, combine):
    folded = tile[:, :LANES]
    for start in range(LANES, tile.shape[1], LANES):
        folded = combine(folded, tile[:, start : start + LANES])
    return folded


def exchange(
    replicas, rows_split, cols_split, matrices,
    delta_ref, tiles_ref, peaks_ref, squares_ref,
    own, peer, stage, peaks, wide, total, mine, from_rep, middle, from_grid,
    own_sem, rep_send, rep_recv, tile_send, tile_recv, peak_send, peak_recv,
    first_send, first_recv, second_send, second_recv, local_sem,
):
    rep, gx, gy = lax.axis_index("rep"), lax.axis_index("gx"), lax.axis_index("gy")
    steps, rows, cols = stage.shape
    grid = rows_split * cols_split
    far = rows_split * (cols_split - 1)
    remote_steps = steps - matrices
    band = total.shape[0]
    here = gx * cols_split + gy

    def place(step):
        turn, matrix = step // matrices, step % matrices
        spread = max(cols_split - 1, 1)
        is_far = turn < far
        row_shift = jnp.where(is_far, turn // spread, (turn - far + 1) % rows_split)
        col_shift = jnp.where(is_far, 1 + (turn % spread + 1) % spread, 0)
        return matrix, (gx + row_shift) % rows_split, (gy + col_shift) % cols_split

    def block(step, replica):
        matrix, c, d = place(step)
        return delta_ref.at[matrix, c, replica, :, pl.ds(pl.multiple_of(d * cols, LANES), cols)]

    def own_copy(step):
        return pltpu.make_async_copy(block(step, rep), own.at[step], own_sem.at[step])

    def rep_copy(shift, step):
        target = (rep + shift) % replicas
        return pltpu.make_async_remote_copy(
            src_ref=block(step, target), dst_ref=peer.at[shift - 1, step],
            send_sem=rep_send.at[shift - 1, step], recv_sem=rep_recv.at[shift - 1, step],
            device_id={"rep": target}, device_id_type=MESH,
        )

    def tile_copies(step):
        matrix, c, d = place(step)
        slot = here * matrices + matrix
        target = {"gx": c, "gy": d}
        return (
            pltpu.make_async_remote_copy(
                src_ref=stage.at[step], dst_ref=tiles_ref.at[matrix, gx, gy],
                send_sem=tile_send.at[step], recv_sem=tile_recv.at[slot],
                device_id=target, device_id_type=MESH,
            ),
            pltpu.make_async_remote_copy(
                src_ref=peaks.at[step], dst_ref=peaks_ref.at[matrix, gx, gy],
                send_sem=peak_send.at[step], recv_sem=peak_recv.at[slot],
                device_id=target, device_id_type=MESH,
            ),
        )

    def neighbour(shift):
        return (gx + shift // cols_split) % rows_split, (gy + shift % cols_split) % cols_split

    barrier = pltpu.get_barrier_semaphore()
    for shift in range(1, replicas):
        pl.semaphore_signal(
            barrier, inc=1, device_id={"rep": (rep + shift) % replicas}, device_id_type=MESH
        )

    def greet(shift, carry):
        c, d = neighbour(shift)
        pl.semaphore_signal(barrier, inc=1, device_id={"gx": c, "gy": d}, device_id_type=MESH)
        return carry

    lax.fori_loop(1, grid, greet, 0)
    pl.semaphore_wait(barrier, replicas - 1 + grid - 1)

    def launch(step):
        own_copy(step).start()
        for shift in range(1, replicas):
            rep_copy(shift, step).start()

    ahead = min(AHEAD, steps)
    lax.fori_loop(0, ahead, lambda step, carry: (launch(step), carry)[1], 0)
    total[...] = jnp.zeros_like(total)

    def advance(step, carry):
        own_copy(step).wait()
        for shift in range(1, replicas):
            rep_copy(shift, step).wait_recv()

        @pl.when(step + ahead < steps)
        def _():
            launch(step + ahead)

        @pl.when((step >= 1) & (step - 1 < remote_steps))
        def _():
            for copy in tile_copies(step - 1):
                copy.start()

        def average(index, peak):
            at = pl.ds(pl.multiple_of(index * band, band), band)
            value = own[step, at, :].astype(jnp.float32)
            for shift in range(1, replicas):
                value = value + peer[shift - 1, step, at, :].astype(jnp.float32)
            value = value * (1.0 / replicas)
            total[...] += value * value
            wide[at, :] = value
            return jnp.maximum(peak, fold_lanes(jnp.abs(value), jnp.maximum))

        peak = lax.fori_loop(0, rows // band, average, jnp.zeros((band, LANES), jnp.float32))
        peak = jnp.maximum(jnp.max(peak, axis=0, keepdims=True), SMALLEST)
        peaks[step] = peak * (1.0 / TOP)
        lift = jnp.concatenate([TOP / peak] * (cols // LANES), axis=1)

        def code(index, carry):
            at = pl.ds(pl.multiple_of(index * band, band), band)
            stage[step, at, :] = encode(wide[at, :] * lift)
            return carry

        lax.fori_loop(0, rows // band, code, 0)
        return carry

    lax.fori_loop(0, steps, advance, 0)

    mine[...] = jnp.sum(fold_lanes(total[...], jnp.add), axis=0, keepdims=True)

    def local_copies(matrix):
        step = remote_steps + matrix
        return (
            pltpu.make_async_copy(stage.at[step], tiles_ref.at[matrix, gx, gy], local_sem.at[matrix, 0]),
            pltpu.make_async_copy(peaks.at[step], peaks_ref.at[matrix, gx, gy], local_sem.at[matrix, 1]),
        )

    def first_copy(shift):
        return pltpu.make_async_remote_copy(
            src_ref=mine, dst_ref=from_rep.at[shift - 1],
            send_sem=first_send.at[shift - 1], recv_sem=first_recv.at[shift - 1],
            device_id={"rep": (rep + shift) % replicas}, device_id_type=MESH,
        )

    def second_copy(shift):
        c, d = neighbour(shift)
        return pltpu.make_async_remote_copy(
            src_ref=middle, dst_ref=from_grid.at[shift - 1],
            send_sem=second_send.at[shift - 1], recv_sem=second_recv.at[shift - 1],
            device_id={"gx": c, "gy": d}, device_id_type=MESH,
        )

    for matrix in range(matrices):
        for copy in local_copies(matrix):
            copy.start()
    for shift in range(1, replicas):
        first_copy(shift).start()
    for matrix in range(matrices):
        for copy in local_copies(matrix):
            copy.wait()
    subtotal = mine[...]
    for shift in range(1, replicas):
        first_copy(shift).wait()
        subtotal = subtotal + from_rep[shift - 1]
    middle[...] = subtotal

    def close_rep(step, carry):
        for shift in range(1, replicas):
            rep_copy(shift, step).wait_send()
        return carry

    lax.fori_loop(0, steps, close_rep, 0)
    lax.fori_loop(1, grid, lambda shift, carry: (second_copy(shift).start(), carry)[1], 0)

    def gather(shift, carry):
        second_copy(shift).wait()
        return carry + from_grid[shift - 1]

    squares_ref[...] = lax.fori_loop(1, grid, gather, subtotal)

    def close_send(step, carry):
        for copy in tile_copies(step):
            copy.wait_send()
        return carry

    lax.fori_loop(0, remote_steps, close_send, 0)

    def close_recv(index, carry):
        c, d = neighbour(1 + index // matrices)
        matrix = index % matrices
        slot = (c * cols_split + d) * matrices + matrix
        target = {"gx": c, "gy": d}
        pltpu.make_async_remote_copy(
            src_ref=stage.at[0], dst_ref=tiles_ref.at[matrix, c, d],
            send_sem=tile_send.at[0], recv_sem=tile_recv.at[slot],
            device_id=target, device_id_type=MESH,
        ).wait_recv()
        pltpu.make_async_remote_copy(
            src_ref=peaks.at[0], dst_ref=peaks_ref.at[matrix, c, d],
            send_sem=peak_send.at[0], recv_sem=peak_recv.at[slot],
            device_id=target, device_id_type=MESH,
        ).wait_recv()
        return carry

    lax.fori_loop(0, remote_steps, close_recv, 0)


def update(entries, squares_ref, tiles_ref, peaks_ref, params_ref, momentum_ref, new_params_ref, new_momentum_ref):
    squares = jnp.sum(squares_ref[...], axis=1, keepdims=True)
    clip_scale = jnp.minimum(1.0, clip_level / jnp.sqrt(squares / entries + epsilon))
    count, rows, cols = tiles_ref.shape
    band = 16 if rows % 16 == 0 else rows
    for tile in range(count):
        lift = jnp.concatenate([peaks_ref[tile] * clip_scale] * (cols // LANES), axis=1)

        def one(index, carry):
            at = pl.ds(pl.multiple_of(index * band, band), band)
            gradient = decode(tiles_ref[tile, at, :]) * lift
            new_momentum = moment_decay * momentum_ref[tile, at, :] + gradient
            new_momentum_ref[tile, at, :] = new_momentum
            new_params_ref[tile, at, :] = params_ref[tile, at, :] - outer_rate * (
                gradient + moment_decay * new_momentum
            )
            return carry

        lax.fori_loop(0, rows // band, one, 0)


def per_device(deltas, params, momentum):
    rows_split = lax.axis_size("gx")
    cols_split = lax.axis_size("gy")
    replicas = lax.axis_size("rep")
    matrices, local_rows, local_cols = deltas.shape[1:]
    rows = local_rows // (rows_split * replicas)
    cols = local_cols // cols_split
    entries = matrices * local_rows * local_cols * rows_split * cols_split
    grid = rows_split * cols_split
    steps = grid * matrices
    remote_steps = steps - matrices
    band = 16 if rows % 16 == 0 else rows
    any_space = pl.BlockSpec(memory_space=pl.ANY)
    vmem = pl.BlockSpec(memory_space=pltpu.VMEM)
    dma = pltpu.SemaphoreType.DMA
    f32, bf16 = jnp.float32, jnp.bfloat16
    padded = -(-rows // 16) * 16
    buffers = (replicas + 1) * steps * padded * cols * 2
    tiles, peaks, squares = pl.pallas_call(
        functools.partial(exchange, replicas, rows_split, cols_split, matrices),
        out_shape=(
            jax.ShapeDtypeStruct((matrices, rows_split, cols_split, rows, cols), bf16),
            jax.ShapeDtypeStruct((matrices, rows_split, cols_split, 1, LANES), f32),
            jax.ShapeDtypeStruct((1, LANES), f32),
        ),
        in_specs=[any_space],
        out_specs=(any_space, any_space, vmem),
        scratch_shapes=[
            pltpu.VMEM((steps, rows, cols), bf16),
            pltpu.VMEM((max(replicas - 1, 1), steps, rows, cols), bf16),
            pltpu.VMEM((steps, rows, cols), bf16),
            pltpu.VMEM((steps, 1, LANES), f32),
            pltpu.VMEM((rows, cols), f32),
            pltpu.VMEM((band, cols), f32),
            pltpu.VMEM((1, LANES), f32),
            pltpu.VMEM((max(replicas - 1, 1), 1, LANES), f32),
            pltpu.VMEM((1, LANES), f32),
            pltpu.VMEM((grid, 1, LANES), f32),
            dma((steps,)),
            dma((max(replicas - 1, 1), steps)),
            dma((max(replicas - 1, 1), steps)),
            dma((steps,)),
            dma((steps,)),
            dma((steps,)),
            dma((steps,)),
            dma((max(replicas - 1, 1),)),
            dma((max(replicas - 1, 1),)),
            dma((grid,)),
            dma((grid,)),
            dma((matrices, 2)),
        ],
        compiler_params=pltpu.CompilerParams(
            collective_id=0, has_side_effects=True, vmem_limit_bytes=buffers + 6 * 1024 * 1024
        ),
    )(deltas.reshape(matrices, rows_split, replicas, rows, local_cols))
    tile_shape = (steps, rows, cols)
    count = 2 if steps % 2 == 0 else 1
    whole = pl.BlockSpec((1, LANES), lambda i: (0, 0))
    tile_block = pl.BlockSpec((count, rows, cols), lambda i: (i, 0, 0))
    peak_block = pl.BlockSpec((count, 1, LANES), lambda i: (i, 0, 0))
    wide_shape = jax.ShapeDtypeStruct(tile_shape, f32)
    new_params, new_momentum = pl.pallas_call(
        functools.partial(update, entries),
        grid=(steps // count,),
        out_shape=(wide_shape, wide_shape),
        in_specs=[whole, tile_block, peak_block, tile_block, tile_block],
        out_specs=(tile_block, tile_block),
        compiler_params=pltpu.CompilerParams(vmem_limit_bytes=16 * 1024 * 1024),
    )(
        squares,
        tiles.reshape(tile_shape),
        peaks.reshape(steps, 1, LANES),
        params.reshape(tile_shape),
        momentum.reshape(tile_shape),
    )
    return (new_params.reshape(params.shape), new_momentum.reshape(momentum.shape))


def solution(mesh):
    placement = P(None, None, "gx", "rep", None, "gy", None, None)
    return jax.shard_map(
        per_device,
        mesh=mesh,
        in_specs=(P("rep", None, "gx", "gy"), placement, placement),
        out_specs=(placement, placement),
        check_vma=False,
    )
```

time: 730 us -> 188 us (0.26)
  blocking collectives: 595 us -> 0 us
  Pallas kernels: 0 us -> 178 us
  local copies, waits for them, and re-layouts: 72.4 us -> 9.29 us
  other arithmetic: 53.1 us -> 0 us
    psum x1 -> x0, blocking collectives: 298 us -> none  [per_device(): lax.psum(jnp.sum(partial_value * partial_value), ('rep', 'gx', 'gy'))]
    all_to_all x2 -> x0, blocking collectives: 297 us -> none  [the longest x1 150 us: per_device(): lax.all_to_all(partial_value, 'gx', split_axis=1, concat_axis=1, tiled=True)]
    pallas_call x0 -> x2, Pallas kernels: none -> 178 us  [the longest x1 160 us: per_device(): pl.pallas_call(functools.partial(exchange, replicas, rows_split, cols_spl...]
    reduce_sum x2 -> x0, other arithmetic: 30.8 us -> none  [the longest x1 15.7 us: per_device(): jnp.sum(partial_value * partial_value)]
    another operation x2 -> x0, local copies, waits for them, and re-layouts: 29.8 us -> none  [per_device(): blocks[None]]
    add x1 -> x0, other arithmetic: 22.3 us -> none  [per_device(): new_momentum = moment_decay * momentum + gradient]
    unnamed x2 -> x6, local copies, waits for them, and re-layouts: 21.4 us -> 9.29 us
    div x1 -> x0, local copies, waits for them, and re-layouts: 10.6 us -> none  [per_device(): partial_value = summed / replicas]
  transfers between devices with their start and end apart: 1 -> 0, of which waited for: 0 -> 0; matrix products, arithmetic and copies ran while one was open for 0% -> 0% of each run, Pallas kernels for 0% -> 0%
where the time goes in v1:
time: 188 us
  Pallas kernels  178 us (95%)
  local copies, waits for them, and re-layouts  9.29 us (5%)
    pallas_call x1, Pallas kernels, per_device(): pl.pallas_call(functools.partial(exchange, replicas, rows_split, cols_spl...  160 us
    pallas_call x1, Pallas kernels, per_device(): pl.pallas_call(functools.partial(update, entries), grid=(steps // count,)...  17.7 us
    unnamed x6, local copies, waits for them, and re-layouts  9.29 us

profile of v1, /device:TPU:0, one launch (start us, length us, event | category | flops | bytes accessed | tf_op | source)
XLA Modules:
  0.0 187.6 jit_solution(13654507386328868734)
XLA Ops:
  0.6 0.0 copy-start
  0.6 4.6 %copy-done = bf16[1,2,896,3584]{3,2,1,0:T(8,128)(2,1)S(1)} copy-done((bf16[1,2,896,3584]{3,2,1,0:T(8,128)(2,1)S(1)}, bf16[1,2,896,3584]{3,2,1,0:T(8,128)(2,1)}, u32[]{:S(2)}) %copy-start) | copy-done | bytes 12845080
  5.3 0.0 copy-start.1
  5.3 160.0 %shard_map.50 = (bf16[2,4,4,112,896]{4,3,2,1,0:T(8,128)(2,1)S(1)}, f32[2,4,4,1,128]{4,3,2,1,0:T(1,128)S(1)}, f32[1,128]{1,0:T(1,128)S(1)}) custom-call(bf16[2,4,2,112,3584]{4,3,2,1,0:T(8,128)(2,1)S(1)} %bitcast.11), custom_call_target="tpu_custom_call" | custom-call | tf_op jit(solution)/shard_map/pallas_call | solution.py:283
  165.3 0.0 copy-done.1
  165.3 0.0 copy-start.2
  165.3 4.6 %copy-done.2 = f32[2,4,1,1,4,1,112,896]{7,6,5,4,3,2,1,0:T(8,128)S(1)} copy-done((f32[2,4,1,1,4,1,112,896]{7,6,5,4,3,2,1,0:T(8,128)S(1)}, f32[2,4,1,1,4,1,112,896]{7,6,5,4,3,2,1,0:T(8,128)}, u32[]{:S(2)}) %copy-start.2) | copy-done | bytes 12845080
  169.9 17.7 %shard_map.51 = (f32[32,112,896]{2,1,0:T(8,128)}, f32[32,112,896]{2,1,0:T(8,128)}) custom-call(f32[1,128]{1,0:T(1,128)S(1)} %get-tuple-element.7.squares_ref, bf16[32,112,896]{2,1,0:T(8,128)(2,1)S(1)} %bitcast.14, f32[32,1,128]{2,1,0:T(1,128)S(1)} %bitcast.15, f32[32,112,896]{2,1,0:T(8,128)S(1)} %bitcast.12, f32[32,112,896]{2,1,0:T(8,128)S(1)} %bitcast.13), custom_call_target="tpu_custom_call" | custom-call | tf_op jit(solution)/shard_map/pallas_call | solution.py:326
Async XLA Ops:
  0.6 4.7 %copy-start = (bf16[1,2,896,3584]{3,2,1,0:T(8,128)(2,1)S(1)}, bf16[1,2,896,3584]{3,2,1,0:T(8,128)(2,1)}, u32[]{:S(2)}) copy-start(bf16[1,2,896,3584]{3,2,1,0:T(8,128)(2,1)} %param.3) | copy-start | bytes 38535172
  5.3 160.0 %copy-start.1 = (f32[2,4,1,1,4,1,112,896]{7,6,5,4,3,2,1,0:T(8,128)S(1)}, f32[2,4,1,1,4,1,112,896]{7,6,5,4,3,2,1,0:T(8,128)}, u32[]{:S(2)}) copy-start(f32[2,4,1,1,4,1,112,896]{7,6,5,4,3,2,1,0:T(8,128)} %param.4) | copy-start | bytes 38535172
  165.3 4.7 %copy-start.2 = (f32[2,4,1,1,4,1,112,896]{7,6,5,4,3,2,1,0:T(8,128)S(1)}, f32[2,4,1,1,4,1,112,896]{7,6,5,4,3,2,1,0:T(8,128)}, u32[]{:S(2)}) copy-start(f32[2,4,1,1,4,1,112,896]{7,6,5,4,3,2,1,0:T(8,128)} %param.5) | copy-start | bytes 38535172

commit v2 on v1

--- a/solution.py
+++ b/solution.py
@@ -16,7 +16,8 @@
 LANES = 128
 TOP = 240.0
 SMALLEST = 1e-30
-AHEAD = 6
+AHEAD = 16
+LARGE = 54 * 1024 * 1024
 
 
 def encode(value):
@@ -28,9 +29,7 @@
 
 def decode(code):
     wide = code.astype(jnp.float32)
-    root = jnp.abs(wide)
-    for _ in range(4):
-        root = lax.rsqrt(root)
+    root = jnp.exp2(jnp.log2(jnp.abs(wide)) * (1.0 / 16.0))
     root = jnp.where(wide == 0.0, 0.0, root)
     return jnp.where(wide < 0.0, -root, root)
 
@@ -132,11 +131,6 @@
         def _():
             launch(step + ahead)
 
-        @pl.when((step >= 1) & (step - 1 < remote_steps))
-        def _():
-            for copy in tile_copies(step - 1):
-                copy.start()
-
         def average(index, peak):
             at = pl.ds(pl.multiple_of(index * band, band), band)
             value = own[step, at, :].astype(jnp.float32)
@@ -158,6 +152,12 @@
             return carry
 
         lax.fori_loop(0, rows // band, code, 0)
+
+        @pl.when(step < remote_steps)
+        def _():
+            for copy in tile_copies(step):
+                copy.start()
+
         return carry
 
     lax.fori_loop(0, steps, advance, 0)
@@ -249,17 +249,14 @@
     for tile in range(count):
         lift = jnp.concatenate([peaks_ref[tile] * clip_scale] * (cols // LANES), axis=1)
 
-        def one(index, carry):
-            at = pl.ds(pl.multiple_of(index * band, band), band)
+        for start in range(0, rows, band):
+            at = slice(start, start + band)
             gradient = decode(tiles_ref[tile, at, :]) * lift
             new_momentum = moment_decay * momentum_ref[tile, at, :] + gradient
             new_momentum_ref[tile, at, :] = new_momentum
             new_params_ref[tile, at, :] = params_ref[tile, at, :] - outer_rate * (
                 gradient + moment_decay * new_momentum
             )
-            return carry
-
-        lax.fori_loop(0, rows // band, one, 0)
 
 
 def per_device(deltas, params, momentum):
@@ -278,8 +275,6 @@
     vmem = pl.BlockSpec(memory_space=pltpu.VMEM)
     dma = pltpu.SemaphoreType.DMA
     f32, bf16 = jnp.float32, jnp.bfloat16
-    padded = -(-rows // 16) * 16
-    buffers = (replicas + 1) * steps * padded * cols * 2
     tiles, peaks, squares = pl.pallas_call(
         functools.partial(exchange, replicas, rows_split, cols_split, matrices),
         out_shape=(
@@ -314,7 +309,7 @@
             dma((matrices, 2)),
         ],
         compiler_params=pltpu.CompilerParams(
-            collective_id=0, has_side_effects=True, vmem_limit_bytes=buffers + 6 * 1024 * 1024
+            collective_id=0, has_side_effects=True, vmem_limit_bytes=LARGE
         ),
     )(deltas.reshape(matrices, rows_split, replicas, rows, local_cols))
     tile_shape = (steps, rows, cols)
@@ -329,7 +324,7 @@
         out_shape=(wide_shape, wide_shape),
         in_specs=[whole, tile_block, peak_block, tile_block, tile_block],
         out_specs=(tile_block, tile_block),
-        compiler_params=pltpu.CompilerParams(vmem_limit_bytes=16 * 1024 * 1024),
+        compiler_params=pltpu.CompilerParams(vmem_limit_bytes=LARGE),
     )(
         squares,
         tiles.reshape(tile_shape),

time: 188 us -> 184 us (0.979)
  local copies, waits for them, and re-layouts: 9.29 us -> 0 us
  Pallas kernels: 178 us -> 183 us
    unnamed x6 -> x0, local copies, waits for them, and re-layouts: 9.29 us -> none
    pallas_call x1, Pallas kernels: 17.7 us -> 26.2 us  [per_device(): pl.pallas_call(functools.partial(update, entries), grid=(steps // count,)...]
    pallas_call x1, Pallas kernels: 160 us -> 157 us  [per_device(): pl.pallas_call(functools.partial(exchange, replicas, rows_split, cols_spl...]
where the time goes in v2:
time: 184 us
  Pallas kernels  183 us (99%)
    pallas_call x1, Pallas kernels, per_device(): pl.pallas_call(functools.partial(exchange, replicas, rows_split, cols_spl...  157 us
    pallas_call x1, Pallas kernels, per_device(): pl.pallas_call(functools.partial(update, entries), grid=(steps // count,)...  26.2 us

profile of v2, /device:TPU:0, one launch (start us, length us, event | category | flops | bytes accessed | tf_op | source)
XLA Modules:
  0.0 183.8 jit_solution(15746523399981148285)
XLA Ops:
  0.6 157.0 %shard_map.50 = (bf16[2,4,4,112,896]{4,3,2,1,0:T(8,128)(2,1)}, f32[2,4,4,1,128]{4,3,2,1,0:T(1,128)}, f32[1,128]{1,0:T(1,128)}) custom-call(bf16[2,4,2,112,3584]{4,3,2,1,0:T(8,128)(2,1)} %bitcast.11), custom_call_target="tpu_custom_call" | custom-call | tf_op jit(solution)/shard_map/pallas_call | solution.py:278
  157.6 26.2 %shard_map.51 = (f32[32,112,896]{2,1,0:T(8,128)}, f32[32,112,896]{2,1,0:T(8,128)}) custom-call(f32[1,128]{1,0:T(1,128)} %get-tuple-element.7.squares_ref, bf16[32,112,896]{2,1,0:T(8,128)(2,1)} %bitcast.14, f32[32,1,128]{2,1,0:T(1,128)} %bitcast.15, f32[32,112,896]{2,1,0:T(8,128)} %bitcast.12, f32[32,112,896]{2,1,0:T(8,128)} %bitcast.13), custom_call_target="tpu_custom_call" | custom-call | tf_op jit(solution)/shard_map/pallas_call | solution.py:321
